TPU v7x, 32 devices: a whole 2x2x4 slice. The times are simulated.
32 devices in a mesh: tm: 8 (over z, x), rows: 4 (over y, core).
Axes of the slice: x: 2, y: 2, z: 4, core: 2. Of those that a mesh axis runs over, the one named last changes fastest.
Arguments:
- initial_warmth: float32 [1024, 1024], P('rows'), may hold values from -6 to 6
- pattern_choice: int32 [16, 8, 8], P('tm'), may hold values from 0 to 7
- dissipation_tables: float32 [8, 128, 128], replicated, may hold values from -6 to 6
- material_label: int32 [8, 8], replicated, may hold values from 0 to 3
- intercept_kappa: float32 [4], replicated, may hold values from 4 to 8
- sensitivity_coef: float32 [4], replicated, may hold values from -0.5 to 0.5
Outputs:
- warmth_trajectory: float32 [16, 1024, 1024], P('tm', 'rows')
All inputs are finite; a program needn't handle non-finite values.
Results may differ from a plain program's by a relative error of at most 0.0003.
Values sent between devices are 32-bit elements; how exact they have to be, the bound alone decides.
A program may use at most 128 MiB of HBM per device.

v0:
```python
import math

import jax
import jax.numpy as jnp
from jax import lax
from jax.sharding import PartitionSpec as P

TILE = 128
ITERS = 2


TIMESTEP_SIZE = 2.0
ALPHA = 0.05
CROSS_WEIGHT = 1.0 / 64.0
HIGHEST = lax.Precision.HIGHEST


def extended(block, sides, width):
    for axis, dim in sides:
        count = lax.axis_size(axis)
        forward = [(i, i + 1) for i in range(count - 1)]
        backward = [(target, source) for source, target in forward]
        low = lax.ppermute(
            lax.slice_in_dim(block, block.shape[dim] - width, None, axis=dim), axis, forward
        )
        high = lax.ppermute(lax.slice_in_dim(block, 0, width, axis=dim), axis, backward)
        block = jnp.concatenate([low, block, high], axis=dim)
    return block


def shifted(block, axis, distance):
    devices = range(lax.axis_size(axis))
    route = [(i - distance, i) for i in devices if i - distance in devices]
    return lax.ppermute(block, axis, route)


def cosine_tables(length):
    modes = jnp.arange(length, dtype=jnp.int32)[:, None]
    cells = jnp.arange(length, dtype=jnp.int32)[None, :]
    phase = modes * (2 * cells + 1) % (4 * length)
    forward = jnp.cos(phase.astype(jnp.float32) * (math.pi / (2 * length)))
    weights = jnp.where(jnp.arange(length) == 0, 1.0, 2.0).astype(jnp.float32) / length
    inverse = forward.T * weights[None, :]
    return (forward, inverse)


def along_last(values, table):
    array_extent = values.shape
    flat = jnp.dot(
        values.reshape(-1, array_extent[-1]),
        table.T,
        precision=HIGHEST,
        preferred_element_type=jnp.float32,
    )
    return flat.reshape(array_extent[:-1] + (table.shape[0],))


def along_rows(values, table):
    return jnp.einsum("kn,afnc->afkc", table, values, precision=HIGHEST)


def fourier_forward(values):
    count = values.shape[0]
    index = jnp.arange(count, dtype=jnp.int32)
    phase = (index[:, None] * index[None, :] % count).astype(jnp.float32) * (2.0 * math.pi / count)
    table = jnp.concatenate([jnp.cos(phase), -jnp.sin(phase)], 0)
    flat = jnp.dot(
        table, values.reshape(count, -1), precision=HIGHEST, preferred_element_type=jnp.float32
    )
    return flat.reshape((2, count) + values.shape[1:])


def fourier_inverse(values):
    count = values.shape[1]
    index = jnp.arange(count, dtype=jnp.int32)
    phase = (index[:, None] * index[None, :] % count).astype(jnp.float32) * (2.0 * math.pi / count)
    table = jnp.concatenate([jnp.cos(phase), -jnp.sin(phase)], 1) / count
    flat = jnp.dot(
        table, values.reshape(2 * count, -1), precision=HIGHEST, preferred_element_type=jnp.float32
    )
    return flat.reshape((count,) + values.shape[2:])


def shifted_solve(spectra, freq_ids, column_ids, total_steps, grid_height, tile_pitch, conduct):
    shrink = ALPHA ** (1.0 / total_steps)
    theta = (freq_ids % total_steps).astype(jnp.float32) * (2.0 * math.pi / total_steps)
    mu_rows = 2.0 - 2.0 * jnp.cos(
        jnp.arange(grid_height).astype(jnp.float32) * (math.pi / grid_height)
    )
    mu_cols = 2.0 - 2.0 * jnp.cos(column_ids.astype(jnp.float32) * (math.pi / tile_pitch))
    real_den = (1.0 - shrink * jnp.cos(theta))[:, None, None] / TIMESTEP_SIZE + conduct * (
        mu_rows[None, :, None] + CROSS_WEIGHT * mu_cols[None, None, :]
    )
    imag_den = (shrink * jnp.sin(theta) / TIMESTEP_SIZE)[:, None, None]
    norm_den = real_den * real_den + imag_den * imag_den
    real_part = spectra[0]
    imag_part = spectra[1]
    solved_re = (real_part * real_den + imag_part * imag_den) / norm_den
    solved_im = (imag_part * real_den - real_part * imag_den) / norm_den
    return jnp.stack([solved_re, solved_im], 0)


def compute_residual(
    warmth_trajectory, initial_warmth, forcing_term, reference_grid, slope_grid, inner_boundaries
):
    extended_grid = extended(warmth_trajectory, (("rows", 1),), 1)
    kappa_local = reference_grid[None] * (1.0 + slope_grid[None] * jnp.tanh(extended_grid))
    upward_current = (
        0.5
        * (kappa_local[:, 1:] + kappa_local[:, :-1])
        * (extended_grid[:, 1:] - extended_grid[:, :-1])
    )
    upward_current = jnp.where(inner_boundaries[None, :, None], upward_current, 0.0)
    centre = extended_grid[:, 1:-1]
    kappa_mid = kappa_local[:, 1:-1]
    lateral_current = CROSS_WEIGHT * (
        0.5 * (kappa_mid[:, :, 1:] + kappa_mid[:, :, :-1]) * (centre[:, :, 1:] - centre[:, :, :-1])
    )
    zero_column = jnp.zeros_like(centre[:, :, :1])
    across = jnp.concatenate([lateral_current, zero_column], 2) - jnp.concatenate(
        [zero_column, lateral_current], 2
    )
    energy_ledger = upward_current[:, 1:] - upward_current[:, :-1] + across
    evolving_warmth = shifted(warmth_trajectory[-1], "tm", 1)
    evolving_warmth = jnp.where(lax.axis_index("tm") == 0, initial_warmth, evolving_warmth)
    former_warmth = jnp.concatenate([evolving_warmth[None], warmth_trajectory[:-1]], 0)
    return forcing_term - (warmth_trajectory - former_warmth) / TIMESTEP_SIZE + energy_ledger


def shards(
    initial_warmth,
    pattern_choice,
    dissipation_tables,
    material_label,
    intercept_kappa,
    sensitivity_coef,
):
    shard_moments = pattern_choice.shape[0]
    slab_tallies, tile_pitch = initial_warmth.shape
    tm_count = lax.axis_size("tm")
    rows_count = lax.axis_size("rows")
    total_steps = shard_moments * tm_count
    grid_height = slab_tallies * rows_count
    tiles_across = tile_pitch // TILE
    first_row = lax.axis_index("rows") * slab_tallies
    local_rows = first_row + jnp.arange(slab_tallies, dtype=jnp.int32)
    chosen = jnp.take(pattern_choice, local_rows // TILE, axis=1)
    pattern_rows = jnp.take(dissipation_tables, local_rows % TILE, axis=1)
    forcing_term = jnp.zeros((shard_moments, slab_tallies, tiles_across, TILE), jnp.float32)
    for pattern in range(dissipation_tables.shape[0]):
        forcing_term = forcing_term + jnp.where(
            (chosen == pattern)[..., None], pattern_rows[pattern][None, :, None, :], 0.0
        )
    forcing_term = forcing_term.reshape(shard_moments, slab_tallies, tile_pitch)
    padded_rows = first_row - 1 + jnp.arange(slab_tallies + 2, dtype=jnp.int32)
    labels = jnp.take(material_label, jnp.clip(padded_rows, 0, grid_height - 1) // TILE, axis=0)
    base_tiles = jnp.zeros(labels.shape, jnp.float32)
    slope_tiles = jnp.zeros(labels.shape, jnp.float32)
    for label in range(intercept_kappa.shape[0]):
        base_tiles = jnp.where(labels == label, intercept_kappa[label], base_tiles)
        slope_tiles = jnp.where(labels == label, sensitivity_coef[label], slope_tiles)
    reference_grid = jnp.repeat(base_tiles, TILE, axis=1)
    slope_grid = jnp.repeat(slope_tiles, TILE, axis=1)
    upper_rows = padded_rows[:-1]
    inner_boundaries = (upper_rows >= 0) & (upper_rows + 1 <= grid_height - 1)
    conduct = jnp.mean(intercept_kappa)
    step_ids = lax.axis_index("tm") * shard_moments + jnp.arange(shard_moments, dtype=jnp.int32)
    amplification = jnp.exp(step_ids.astype(jnp.float32) * (math.log(ALPHA) / total_steps))
    column_fwd, column_inv = cosine_tables(tile_pitch)
    row_fwd, row_inv = cosine_tables(grid_height)
    narrow = tile_pitch // (tm_count * rows_count)
    arrival = jnp.arange(tile_pitch, dtype=jnp.int32)
    strip_of = arrival // (tm_count * narrow)
    block_of = arrival // narrow % tm_count
    mode_order = block_of * (rows_count * narrow) + strip_of * narrow + arrival % narrow
    column_back = jnp.take(column_inv, mode_order, axis=1)
    warmth_trajectory = jnp.broadcast_to(
        initial_warmth[None], (shard_moments, slab_tallies, tile_pitch)
    )
    for sweep in range(ITERS):
        defect_vector = compute_residual(
            warmth_trajectory,
            initial_warmth,
            forcing_term,
            reference_grid,
            slope_grid,
            inner_boundaries,
        )
        scaled = defect_vector * amplification[:, None, None]
        column_modes = along_last(scaled, column_fwd)
        gathered = lax.all_to_all(
            lax.all_to_all(column_modes, "tm", split_axis=2, concat_axis=0, tiled=True),
            "rows",
            split_axis=2,
            concat_axis=1,
            tiled=True,
        )
        column_width = gathered.shape[2]
        column_ids = (
            lax.axis_index("tm") * (rows_count * column_width)
            + lax.axis_index("rows") * column_width
            + jnp.arange(column_width, dtype=jnp.int32)
        )
        spectra = along_rows(fourier_forward(gathered), row_fwd)
        freq_ids = jnp.arange(total_steps, dtype=jnp.int32)
        solved = shifted_solve(
            spectra, freq_ids, column_ids, total_steps, grid_height, tile_pitch, conduct
        )
        solved = along_rows(solved, row_inv)
        field = fourier_inverse(solved)
        correction_delta = lax.all_to_all(
            lax.all_to_all(field, "tm", split_axis=0, concat_axis=2, tiled=True),
            "rows",
            split_axis=1,
            concat_axis=2,
            tiled=True,
        )
        correction_delta = along_last(correction_delta, column_back)
        warmth_trajectory = warmth_trajectory + correction_delta / amplification[:, None, None]
    return warmth_trajectory


def solution(mesh):
    in_specs = (P("rows", None), P("tm", None, None), P(), P(), P(), P())
    out_specs = P("tm", "rows", None)
    return jax.shard_map(shards, mesh=mesh, in_specs=in_specs, out_specs=out_specs, check_vma=False)
```

profile of v0, /device:TPU:0, one launch (start us, length us, event | category | flops | bytes accessed | tf_op | source)
XLA Modules:
  0.0 817.1 jit_solution(5478636304248418031)
XLA Ops:
  0.0 6.0 collective-permute-start
  12.4 2.9 subtract_multiply_fusion
  15.9 2.4 gather_fusion.1
  31.0 2.1 broadcast_in_dim.320
  41.0 1.9 broadcast_in_dim.344
  43.0 2.2 broadcast_in_dim.345
  45.2 1.9 broadcast_in_dim.350
  47.2 2.2 broadcast_in_dim.351
  49.4 1.9 broadcast_in_dim.356
  51.3 2.2 broadcast_in_dim.357
  55.9 2.6 select_select_fusion.1
  58.6 2.7 select_select_fusion
  61.3 5.9 select_add_fusion
  75.1 26.0 %fusion.29 = f32[2,256,1024]{2,1,0:T(8,128)} fusion(f32[2,257,1024]{2,1,0:T(8,128)S(1)} %fusion.46, f32[2,256,1024]{2,1,0:T(8,128)S(1)} %copy-done.13, f32[1,256,1024]{2,1,0:T(8,128)S(1)} %bitcast.225, f32[1,256,1024]{2,1,0:T(8,128)S(1)} %select_bitcast_fusion.2, s32[1024]{0:T(1024)S(1)} %copy-done.15, f32[2,256,1023]{2,1,0:T(8,128)S(1)} %fusion.91, ...), kind=kOutput, calls=%fused_computation.44 | convolution fusion | flops 6461849600 | bytes 13636096 | tf_op jit(solution)/shard_map/dot_general | solution.py:49
  101.0 2.8 copy.60
  103.9 52.3 %all_to_all.132 = f32[2,256,1024]{1,0,2:T(2,128)S(1)} all-to-all(f32[2,256,1024]{1,0,2:T(2,128)S(1)} %copy.60), channel_id=1, replica_groups=mesh['tm'=8,'rows'=4] {'tm'}, dimensions={2} | all-to-all | bytes 4194304 | tf_op jit(solution)/shard_map/all_to_all | solution.py:192
  156.4 1.8 copy.62
  158.2 3.1 copy.63
  161.3 4.6 all-to-all-start.1
  167.6 23.9 %all-to-all-done.1 = f32[16,256,128]{1,0,2:T(8,128)S(1)} async-done(((f32[16,256,128]{1,0,2:T(8,128)}), f32[16,256,128]{1,0,2:T(8,128)S(1)}, u32[]{:S(2)}, u32[]{:S(2)}) %all-to-all-start.1) | async-done | bytes 2097184 | tf_op jit(solution)/shard_map/all_to_all | solution.py:191
  191.6 4.7 copy.65
  196.2 6.0 reshape.506
  202.2 4.8 dot_general.61
  207.1 5.5 copy.66
  212.5 3.4 fusion.109
  215.9 33.4 %fusion.53 = f32[2,16,1024,32]{2,3,1,0:T(8,128)S(1)} fusion(f32[2,16,1024,32]{2,1,3,0:T(8,128)S(1)} %fusion.109, s32[1024]{0:T(1024)S(1)} %copy-done.15), kind=kOutput, calls=%fused_computation.74 | convolution fusion | flops 12899581952 | bytes 8392704 | tf_op jit(solution)/shard_map/kn,afnc->afkc/dot_general | solution.py:59
  250.5 30.6 %fusion.68 = f32[2,16,1024,32]{2,3,1,0:T(8,128)} fusion(f32[1,16,1024,32]{2,3,1,0:T(8,128)S(1)} %get-tuple-element.13, f32[1,16,1024,32]{2,3,1,0:T(8,128)S(1)} %get-tuple-element.12, f32[1024]{0:T(1024)S(1)} %select_multiply_fusion, s32[1024]{0:T(1024)S(1)} %copy-done.15), kind=kOutput, calls=%fused_computation.77 | convolution fusion | flops 12901679104 | bytes 8396800 | tf_op jit(solution)/shard_map/kn,afnc->afkc/dot_general | solution.py:59
  281.2 10.4 %copy.69 = f32[2,16,1024,32]{3,2,1,0:T(8,128)} copy(f32[2,16,1024,32]{2,3,1,0:T(8,128)} %fusion.68) | data formatting | bytes 8388608 | tf_op jit(solution)/shard_map/kn,afnc->afkc/transpose | solution.py:59
  291.6 11.6 %reshape.507 = f32[32,32768]{1,0:T(8,128)} reshape(f32[2,16,1024,32]{3,2,1,0:T(8,128)} %copy.69) | data formatting | bytes 8388608 | tf_op jit(solution)/shard_map/reshape | solution.py:79
  303.3 9.8 %dot_general.66 = f32[1024,32,32]{1,0,2:T(8,128)} reshape(f32[32768,32]{0,1:T(8,128)} %bitcast.226) | data formatting | bytes 8388608 | tf_op jit(solution)/shard_map/dot_general | solution.py:78
  313.1 11.8 %copy.70 = f32[1024,32,32]{0,2,1:T(8,128)} copy(f32[1024,32,32]{1,0,2:T(8,128)} %dot_general.66) | data formatting | bytes 8388608 | tf_op jit(solution)/shard_map/dot_general | solution.py:78
  324.9 4.1 fusion.165
  330.3 51.1 %all_to_all.133 = f32[16,1024,32]{1,2,0:T(8,128)S(1)} all-to-all(f32[16,1024,32]{1,2,0:T(8,128)S(1)} %copy.71), channel_id=1, replica_groups=mesh['tm'=8,'rows'=4] {'tm'}, dimensions={0} | all-to-all | bytes 4194304 | tf_op jit(solution)/shard_map/all_to_all | solution.py:212
  381.6 2.4 copy.73
  384.0 4.0 all-to-all-start.3
  388.1 16.2 %fusion.8 = f32[1024,1024]{0,1:T(8,128)} fusion(f32[1024]{0:T(1024)S(1)} %select_multiply_fusion, s32[1024]{0:T(1024)S(1)} %copy-done.15), kind=kLoop, calls=%fused_computation.23 | loop fusion | flops 15728640 | bytes 4202496 | tf_op jit(solution)/shard_map/mul | solution.py:43
  404.3 8.5 %gather_fusion.3 = f32[1024,1024]{1,0:T(8,128)} fusion(f32[1024,1024]{0,1:T(8,128)} %fusion.8, s32[1024]{0:T(1024)S(1)} %broadcast_clamp_fusion), kind=kCustom, calls=%fused_computation.3 | custom fusion | bytes 8392704 | tf_op jit(solution)/shard_map/jit(_take)/gather | solution.py:176
  416.2 7.3 divide_add_fusion.1
  423.5 1.7 collective-permute-start.4
  426.7 3.5 collective-permute-start.3
  432.7 19.5 %collective-permute-done.3 = f32[256,1024]{1,0:T(8,128)S(1)} collective-permute-done((f32[256,1024]{1,0:T(8,128)S(1)}, f32[256,1024]{1,0:T(8,128)S(1)}, u32[]{:S(2)}, u32[]{:S(2)}) %collective-permute-start.3) | collective-permute-done | bytes 1048608 | tf_op jit(solution)/shard_map/ppermute | solution.py:34
  452.4 25.7 %fusion.27 = f32[2,256,1024]{2,1,0:T(8,128)} fusion(f32[2,257,1024]{2,1,0:T(8,128)S(1)} %fusion.43, f32[2,256,1024]{2,1,0:T(8,128)S(1)} %copy-done.14, f32[2,256,1024]{2,1,0:T(8,128)S(1)} %divide_add_fusion.1, f32[1,256,1024]{2,1,0:T(8,128)S(1)} %get-tuple-element.15, f32[1,256,1024]{2,1,0:T(8,128)S(1)} %select_bitcast_fusion.1, ...), kind=kOutput, calls=%fused_computation.42 | convolution fusion | flops 6461849600 | bytes 14684672 | tf_op jit(solution)/shard_map/dot_general | solution.py:49
  478.2 4.1 copy.77
  482.3 54.1 %all_to_all.134 = f32[2,256,1024]{1,0,2:T(2,128)S(1)} all-to-all(f32[2,256,1024]{1,0,2:T(2,128)} %copy.77), channel_id=1, replica_groups=mesh['tm'=8,'rows'=4] {'tm'}, dimensions={2} | all-to-all | bytes 4194304 | tf_op jit(solution)/shard_map/all_to_all | solution.py:192
  537.9 2.9 copy.79
  540.8 3.0 copy.80
  543.8 30.4 %all_to_all.135 = f32[16,256,128]{1,0,2:T(8,128)} all-to-all(f32[16,256,128]{1,0,2:T(8,128)} %copy.80), channel_id=1, replica_groups=mesh['tm'=8,'rows'=4] {'rows'}, dimensions={2} | all-to-all | bytes 4194304 | tf_op jit(solution)/shard_map/all_to_all | solution.py:191
  574.2 6.3 copy.82
  580.5 7.0 reshape.508
  587.5 6.0 dot_general.72
  593.5 6.4 copy.83
  599.9 5.0 fusion.107
  604.9 33.5 %fusion.58 = f32[2,16,1024,32]{2,3,1,0:T(8,128)S(1)} fusion(f32[2,16,1024,32]{2,1,3,0:T(8,128)S(1)} %fusion.107, s32[1024]{0:T(1024)S(1)} %copy-done.15), kind=kOutput, calls=%fused_computation.75 | convolution fusion | flops 12899581952 | bytes 8392704 | tf_op jit(solution)/shard_map/kn,afnc->afkc/dot_general | solution.py:59
  639.5 30.6 %fusion.63 = f32[2,16,1024,32]{2,3,1,0:T(8,128)} fusion(f32[1,16,1024,32]{2,3,1,0:T(8,128)S(1)} %get-tuple-element.11, f32[1,16,1024,32]{2,3,1,0:T(8,128)S(1)} %get-tuple-element.10, f32[1024]{0:T(1024)S(1)} %select_multiply_fusion, s32[1024]{0:T(1024)S(1)} %copy-done.15), kind=kOutput, calls=%fused_computation.76 | convolution fusion | flops 12901679104 | bytes 8396800 | tf_op jit(solution)/shard_map/kn,afnc->afkc/dot_general | solution.py:59
  670.2 10.4 %copy.86 = f32[2,16,1024,32]{3,2,1,0:T(8,128)} copy(f32[2,16,1024,32]{2,3,1,0:T(8,128)} %fusion.63) | data formatting | bytes 8388608 | tf_op jit(solution)/shard_map/kn,afnc->afkc/transpose | solution.py:59
  680.6 11.7 %reshape.509 = f32[32,32768]{1,0:T(8,128)} reshape(f32[2,16,1024,32]{3,2,1,0:T(8,128)} %copy.86) | data formatting | bytes 8388608 | tf_op jit(solution)/shard_map/reshape | solution.py:79
  692.4 9.8 %dot_general.77 = f32[1024,32,32]{1,0,2:T(8,128)} reshape(f32[32768,32]{0,1:T(8,128)} %bitcast.227) | data formatting | bytes 8388608 | tf_op jit(solution)/shard_map/dot_general | solution.py:78
  702.2 11.8 %copy.87 = f32[1024,32,32]{0,2,1:T(8,128)} copy(f32[1024,32,32]{1,0,2:T(8,128)} %dot_general.77) | data formatting | bytes 8388608 | tf_op jit(solution)/shard_map/dot_general | solution.py:78
  714.0 4.1 fusion.163
  719.4 51.5 %all_to_all.136 = f32[16,1024,32]{1,2,0:T(8,128)S(1)} all-to-all(f32[16,1024,32]{1,2,0:T(8,128)S(1)} %copy.88), channel_id=1, replica_groups=mesh['tm'=8,'rows'=4] {'tm'}, dimensions={0} | all-to-all | bytes 4194304 | tf_op jit(solution)/shard_map/all_to_all | solution.py:212
  772.3 4.1 copy.90
  776.4 29.5 %all_to_all.137 = f32[2,1024,256]{2,0,1:T(2,128)S(1)} all-to-all(f32[2,1024,256]{2,0,1:T(2,128)} %copy.90), channel_id=1, replica_groups=mesh['tm'=8,'rows'=4] {'rows'}, dimensions={1} | all-to-all | bytes 4194304 | tf_op jit(solution)/shard_map/all_to_all | solution.py:211
  806.3 1.9 copy-done.11
  808.2 8.6 %divide_add_fusion = f32[2,256,1024]{2,1,0:T(8,128)} fusion(f32[2,256,1024]{2,1,0:T(8,128)S(1)} %divide_add_fusion.1, f32[2]{0:T(128)S(1)} %multiply_exponential_fusion, f32[2,256,1024]{2,1,0:T(8,128)S(1)} %bitcast.264, f32[1024,1024]{1,0:T(8,128)S(1)} %copy-done.11, pred[1024]{0:T(1024)(128)(4,1)S(1)} %compare_and_fusion), kind=kOutput, calls=%fused_computation.121 | convolution fusion | flops 6444548096 | bytes 10486792 | tf_op jit(solution)/shard_map/dot_general | solution.py:49
  (137 shorter events, 54.4 us)
Async XLA Ops:
  0.0 15.9 %copy-start = (f32[8,128,128]{2,1,0:T(8,128)S(1)}, f32[8,128,128]{2,1,0:T(8,128)}, u32[]{:S(2)}) copy-start(f32[8,128,128]{2,1,0:T(8,128)} %param.8) | copy-start | bytes 1572868
  0.0 73.5 %collective-permute-start = (f32[256,1024]{1,0:T(8,128)}, f32[256,1024]{1,0:T(8,128)}, u32[]{:S(2)}, u32[]{:S(2)}) collective-permute-start(f32[256,1024]{1,0:T(8,128)} %param.6), channel_id=1, source_target_pairs={{0,4},{4,8},{8,12},{12,16},{16,20},{20,24},{24,28},{1,5},{5,9},{9,... | collective-permute-start | bytes 3145736 | tf_op jit(solution)/shard_map/ppermute | solution.py:34
  7.4 62.2 %collective-permute-start.1 = (f32[2,1,1024]{2,1,0:T(1,128)}, f32[2,1,1024]{2,1,0:T(1,128)S(1)}, u32[]{:S(2)}, u32[]{:S(2)}) collective-permute-start(f32[2,1,1024]{2,1,0:T(1,128)} %broadcast_in_dim.376), channel_id=1, source_target_pairs={{0,1},{1,2},{2,3},{4,5},{5,6},{6,7},{8,9},{9,10},{10,11},{12,13},{... | collective-permute-start | bytes 24584 | tf_op jit(solution)/shard_map/ppermute | solution.py:23
  9.4 60.1 %collective-permute-start.2 = (f32[2,1,1024]{2,1,0:T(1,128)}, f32[2,1,1024]{2,1,0:T(1,128)S(1)}, u32[]{:S(2)}, u32[]{:S(2)}) collective-permute-start(f32[2,1,1024]{2,1,0:T(1,128)} %broadcast_in_dim.377), channel_id=1, source_target_pairs={{1,0},{2,1},{3,2},{5,4},{6,5},{7,6},{9,8},{10,9},{11,10},{13,12},{... | collective-permute-start | bytes 24584 | tf_op jit(solution)/shard_map/ppermute | solution.py:26
  25.5 1.4 copy-start.2
  42.9 10.6 %copy-start.16 = (s32[258]{0:T(512)S(1)}, s32[258]{0:T(512)}, u32[]{:S(2)}) copy-start(s32[258]{0:T(512)} %fusion.170) | copy-start | bytes 3100
  42.9 10.6 %copy-start.19 = (f32[4]{0:T(128)S(1)}, f32[4]{0:T(128)}, u32[]{:S(2)}) copy-start(f32[4]{0:T(128)} %param.10) | copy-start | bytes 52
  42.9 11.2 %copy-start.18 = (f32[4]{0:T(128)S(1)}, f32[4]{0:T(128)}, u32[]{:S(2)}) copy-start(f32[4]{0:T(128)} %param.11) | copy-start | bytes 52
  42.9 11.9 %copy-start.17 = (s32[258]{0:T(512)S(1)}, s32[258]{0:T(512)}, u32[]{:S(2)}) copy-start(s32[258]{0:T(512)} %iota_add_fusion) | copy-start | bytes 3100
  43.0 11.9 %copy-start.3 = (s32[8,8]{1,0:T(8,128)S(1)}, s32[8,8]{1,0:T(8,128)}, u32[]{:S(2)}) copy-start(s32[8,8]{1,0:T(8,128)} %param.9) | copy-start | bytes 772
  45.2 10.7 %copy-start.20 = (pred[258]{0:T(512)(128)(4,1)S(1)}, pred[258]{0:T(512)(128)(4,1)}, u32[]{:S(2)}) copy-start(pred[258]{0:T(512)(128)(4,1)} %compare_and_fusion.1) | copy-start | bytes 778
  67.8 2.0 copy-start.6
  68.2 1.4 copy-start.4
  69.5 1.2 copy-start.8
  70.8 1.2 copy-start.12
  73.5 1.6 copy-start.13
  73.5 1.6 copy-start.15
  161.3 30.2 %all-to-all-start.1 = ((f32[16,256,128]{1,0,2:T(8,128)}), f32[16,256,128]{1,0,2:T(8,128)S(1)}, u32[]{:S(2)}, u32[]{:S(2)}) async-start(f32[16,256,128]{1,0,2:T(8,128)} %copy.63), calls=%async_computation.1 | async-start | bytes 4194304 | tf_op jit(solution)/shard_map/all_to_all | solution.py:191
  384.0 29.6 %all-to-all-start.3 = ((f32[2,1024,256]{2,0,1:T(2,128)}), f32[2,1024,256]{2,0,1:T(2,128)S(1)}, u32[]{:S(2)}, u32[]{:S(2)}) async-start(f32[2,1024,256]{2,0,1:T(2,128)} %copy.73), calls=%async_computation.3 | async-start | bytes 4194304 | tf_op jit(solution)/shard_map/all_to_all | solution.py:211
  413.7 2.2 copy-start.10
  413.8 2.4 copy-start.5
  423.5 6.8 copy-start.7
  423.5 6.8 copy-start.9
  423.5 6.7 collective-permute-start.4
  425.3 5.0 collective-permute-start.5
  426.7 25.5 %collective-permute-start.3 = (f32[256,1024]{1,0:T(8,128)S(1)}, f32[256,1024]{1,0:T(8,128)S(1)}, u32[]{:S(2)}, u32[]{:S(2)}) collective-permute-start(f32[256,1024]{1,0:T(8,128)S(1)} %get-tuple-element.14), channel_id=1, source_target_pairs={{0,4},{4,8},{8,12},{12,16},{16,20},{20,24},{24,28},{1,5},{5,9},{9,... | collective-permute-start | bytes 3145736 | tf_op jit(solution)/shard_map/ppermute | solution.py:34
  432.7 19.7 %copy-start.14 = (f32[2,256,1024]{2,1,0:T(8,128)S(1)}, f32[2,256,1024]{2,1,0:T(8,128)}, u32[]{:S(2)}) copy-start(f32[2,256,1024]{2,1,0:T(8,128)} %select_add_fusion) | copy-start | bytes 6291460
  806.0 2.2 copy-start.11
  808.2 8.6 %copy-start.1 = (f32[8,128,128]{2,1,0:T(8,128)S(1)}, f32[8,128,128]{2,1,0:T(8,128)}, u32[]{:S(2)}) copy-start(f32[8,128,128]{2,1,0:T(8,128)} %param.8) | copy-start | bytes 1572868
where the time goes:
time: 824 us; the launch traced here: 817 us
  blocking collectives  269 us (33%)
  local copies, waits for them, and re-layouts  224 us (27%)
  matrix products  212 us (26%)
  waiting for transfers between devices  44.3 us (5%)
  other arithmetic  42 us (5%)
  starting transfers between devices  23.8 us (3%)
    dot_general x4, matrix products, along_rows(): return jnp.einsum('kn,afnc->afkc', table, values, precision=HIGHEST)  128 us
    all_to_all x2, blocking collectives, shards(): lax.all_to_all(column_modes, 'tm', split_axis=2, concat_axis=0, tiled=True)  106 us
    all_to_all x2, blocking collectives, shards(): lax.all_to_all(field, 'tm', split_axis=0, concat_axis=2, tiled=True)  103 us
    dot_general x4, matrix products, along_last(): jnp.dot(values.reshape(-1, array_extent[-1]), table.T, precision=HIGHEST,...  67.6 us
    dot_general x6, local copies, waits for them, and re-layouts, fourier_inverse(): jnp.dot(table, values.reshape(2 * count, -1), precision=HIGHEST, preferre...  45.7 us
    all_to_all x1, blocking collectives, shards(): lax.all_to_all(lax.all_to_all(column_modes, 'tm', split_axis=2, concat_ax...  30.4 us
    all_to_all x1, blocking collectives, shards(): lax.all_to_all(lax.all_to_all(field, 'tm', split_axis=0, concat_axis=2, t...  29.5 us
    broadcast_in_dim x25, local copies, waits for them, and re-layouts, shards(): jnp.where((chosen == pattern)[..., None], pattern_rows[pattern][None, :,...  25.2 us
  transfers between devices with their start and end apart: 8, of which 3 were waited for; matrix products, arithmetic and copies ran while one was open for 11% of the time, Pallas kernels for 0%

commit v1 on v0

v1 whole, which is shorter than its diff:
```python
import math

import jax
import jax.numpy as jnp
import numpy as np
from jax import lax
from jax.experimental import pallas as pl
from jax.experimental.pallas import tpu as pltpu
from jax.sharding import PartitionSpec as P

TILE = 128
ITERS = 2
TIMESTEP_SIZE = 2.0
ALPHA = 0.05
CROSS_WEIGHT = 1.0 / 64.0
F32 = jnp.float32
BF16 = jnp.bfloat16


def extended(block, axis, dim):
    count = lax.axis_size(axis)
    forward = [(i, i + 1) for i in range(count - 1)]
    backward = [(target, source) for source, target in forward]
    low = lax.ppermute(
        lax.slice_in_dim(block, block.shape[dim] - 1, None, axis=dim), axis, forward
    )
    high = lax.ppermute(lax.slice_in_dim(block, 0, 1, axis=dim), axis, backward)
    return jnp.concatenate([low, block, high], axis=dim)


def cosine_table(length):
    modes = np.arange(length, dtype=np.int64)[:, None]
    cells = np.arange(length, dtype=np.int64)[None, :]
    phase = modes * (2 * cells + 1) % (4 * length)
    return np.cos(phase * (math.pi / (2 * length)))


def two_parts(table):
    high = np.asarray(table, dtype=np.float32).astype(BF16)
    low = (table - high.astype(np.float64)).astype(np.float32).astype(BF16)
    return jnp.asarray(high), jnp.asarray(low)


def split(values):
    high = values.astype(BF16)
    return high, (values - high.astype(F32)).astype(BF16)


def mul(left, right):
    return jnp.dot(left, right, preferred_element_type=F32)


def columns_kernel(x_ref, high_ref, low_ref, out_ref, x_high, x_low):
    @pl.when(pl.program_id(0) == 0)
    def _():
        x_high[...], x_low[...] = split(x_ref[...])

    high = high_ref[...]
    out_ref[...] = (
        mul(x_high[...], high) + mul(x_low[...], high) + mul(x_high[...], low_ref[...])
    )


def times_table(values, table):
    rows, depth = values.shape
    width = table[0].shape[1]
    block = min(256, width)
    return pl.pallas_call(
        columns_kernel,
        grid=(width // block,),
        out_shape=jax.ShapeDtypeStruct((rows, width), F32),
        in_specs=[
            pl.BlockSpec((rows, depth), lambda i: (0, 0)),
            pl.BlockSpec((depth, block), lambda i: (0, i)),
            pl.BlockSpec((depth, block), lambda i: (0, i)),
        ],
        out_specs=pl.BlockSpec((rows, block), lambda i: (0, i)),
        scratch_shapes=[pltpu.VMEM((rows, depth), BF16)] * 2,
    )(values, *table)


def rows_kernel(high_ref, low_ref, x_ref, out_ref, x_high, x_low):
    @pl.when(pl.program_id(0) == 0)
    def _():
        x_high[...], x_low[...] = split(x_ref[...])

    for n in range(x_ref.shape[0]):
        out_ref[n] = (
            mul(high_ref[...], x_high[n])
            + mul(high_ref[...], x_low[n])
            + mul(low_ref[...], x_high[n])
        )


def table_times(table, values):
    steps, depth, width = values.shape
    height = table[0].shape[0]
    block = min(256, height)
    return pl.pallas_call(
        rows_kernel,
        grid=(height // block,),
        out_shape=jax.ShapeDtypeStruct((steps, height, width), F32),
        in_specs=[
            pl.BlockSpec((block, depth), lambda i: (i, 0)),
            pl.BlockSpec((block, depth), lambda i: (i, 0)),
            pl.BlockSpec((steps, depth, width), lambda i: (0, 0, 0)),
        ],
        out_specs=pl.BlockSpec((steps, block, width), lambda i: (0, i, 0)),
        scratch_shapes=[pltpu.VMEM((steps, depth, width), BF16)] * 2,
    )(*table, values)


def power_kernel(choice_ref, table_ref, out_ref):
    steps, blocks, _, width = out_ref.shape
    across = width // TILE
    for n in range(steps):
        for b in range(blocks):
            for x in range(across):
                picked = choice_ref[n, b * across + x]
                out_ref[n, b, :, x * TILE : (x + 1) * TILE] = table_ref[picked]


def power_of(pattern_choice, tables, first_row, strip, width):
    steps = pattern_choice.shape[0]
    part = min(TILE, strip)
    blocks = strip // part
    offset = first_row % TILE if strip < TILE else 0
    tiles = lax.dynamic_slice_in_dim(tables, offset, part, axis=1)
    chosen = lax.dynamic_slice_in_dim(pattern_choice, first_row // TILE, blocks, axis=1)
    power = pl.pallas_call(
        power_kernel,
        out_shape=jax.ShapeDtypeStruct((steps, blocks, part, width), F32),
        in_specs=[
            pl.BlockSpec(memory_space=pltpu.SMEM),
            pl.BlockSpec(memory_space=pltpu.VMEM),
        ],
        out_specs=pl.BlockSpec(memory_space=pltpu.VMEM),
    )(chosen.reshape(steps, -1), tiles)
    return power.reshape(steps, strip, width)


def divergence(warmth, kappa, inner):
    def face(low, high):
        return 1.0 if kappa is None else 0.5 * (low + high)

    k = warmth if kappa is None else kappa
    upward = face(k[:, 1:], k[:, :-1]) * (warmth[:, 1:] - warmth[:, :-1])
    upward = jnp.where(inner[None, :, None], upward, 0.0)
    centre, k_mid = warmth[:, 1:-1], k[:, 1:-1]
    lateral = CROSS_WEIGHT * (
        face(k_mid[:, :, 1:], k_mid[:, :, :-1]) * (centre[:, :, 1:] - centre[:, :, :-1])
    )
    zero = jnp.zeros_like(centre[:, :, :1])
    across = jnp.concatenate([lateral, zero], 2) - jnp.concatenate([zero, lateral], 2)
    return upward[:, 1:] - upward[:, :-1] + across


def mode_factors(row_ids, column_ids, height, width, conduct):
    mu_rows = 2.0 - 2.0 * jnp.cos(row_ids.astype(F32) * (math.pi / height))
    mu_cols = 2.0 - 2.0 * jnp.cos(column_ids.astype(F32) * (math.pi / width))
    rate = conduct * (mu_rows[:, None] + CROSS_WEIGHT * mu_cols[None, :])
    gain = 1.0 / (1.0 / TIMESTEP_SIZE + rate)
    return gain, gain * (1.0 / TIMESTEP_SIZE)


def shards(
    initial_warmth,
    pattern_choice,
    dissipation_tables,
    material_label,
    intercept_kappa,
    sensitivity_coef,
):
    steps = pattern_choice.shape[0]
    strip, width = initial_warmth.shape
    tm_count = lax.axis_size("tm")
    rows_count = lax.axis_size("rows")
    height = strip * rows_count
    first_row = lax.axis_index("rows") * strip
    power = power_of(pattern_choice, dissipation_tables, first_row, strip, width)

    padded_rows = first_row - 1 + jnp.arange(strip + 2, dtype=jnp.int32)
    labels = jnp.take(material_label, jnp.clip(padded_rows, 0, height - 1) // TILE, axis=0)
    base_tiles = jnp.zeros(labels.shape, F32)
    slope_tiles = jnp.zeros(labels.shape, F32)
    for label in range(intercept_kappa.shape[0]):
        base_tiles = jnp.where(labels == label, intercept_kappa[label], base_tiles)
        slope_tiles = jnp.where(labels == label, sensitivity_coef[label], slope_tiles)
    base = jnp.repeat(base_tiles, TILE, axis=1)[None]
    slope = jnp.repeat(slope_tiles, TILE, axis=1)[None]
    upper_rows = padded_rows[:-1]
    inner = (upper_rows >= 0) & (upper_rows + 1 <= height - 1)
    conduct = jnp.mean(intercept_kappa)

    column_cos = cosine_table(width)
    row_cos = cosine_table(height)
    columns_out, columns_in = two_parts(column_cos.T), two_parts(column_cos)
    if height == width:
        rows_out, rows_in = columns_in, columns_out
    else:
        rows_out, rows_in = two_parts(row_cos), two_parts(row_cos.T)

    narrow = width // rows_count
    share = height // tm_count
    column_ids = lax.axis_index("rows") * narrow + jnp.arange(narrow, dtype=jnp.int32)
    all_rows = jnp.arange(height, dtype=jnp.int32)
    own_rows = lax.axis_index("tm") * share + jnp.arange(share, dtype=jnp.int32)
    gain, keep = mode_factors(all_rows, column_ids, height, width, conduct)
    weight = (jnp.where(all_rows == 0, 1.0, 2.0) / height)[:, None] * (
        jnp.where(column_ids == 0, 1.0, 2.0) / width
    )[None, :]
    _, own_keep = mode_factors(own_rows, column_ids, height, width, conduct)
    block_keep = own_keep
    for _ in range(steps - 1):
        block_keep = block_keep * own_keep
    around = block_keep
    for _ in range(tm_count - 1):
        around = around * block_keep
    closing = ALPHA / (1.0 - ALPHA * around)
    first_block = lax.axis_index("tm") == 0

    start = extended(initial_warmth[None], "rows", 1)
    start_div = divergence(start, base * (1.0 + slope * jnp.tanh(start)), inner)
    warmth = jnp.broadcast_to(initial_warmth[None], (steps, strip, width))
    wrapped = None
    for sweep in range(ITERS):
        if sweep == 0:
            resid = power + start_div
        else:
            grid = extended(warmth, "rows", 1)
            div = divergence(grid, base * (1.0 + slope * jnp.tanh(grid)), inner)
            resid = div - last_div - conduct * divergence(grid - last_grid, None, inner)
        modes = times_table(resid.reshape(steps * strip, width), columns_out)
        modes = lax.all_to_all(
            modes.reshape(steps, strip, width), "rows", split_axis=2, concat_axis=1, tiled=True
        )
        modes = table_times(rows_out, modes)
        sources = [modes[n] * weight for n in range(steps)]
        if wrapped is not None:
            sources[0] = sources[0] - jnp.where(first_block, wrapped / TIMESTEP_SIZE, 0.0)
        sources = [gain * source for source in sources]
        block_end = sources[0]
        for source in sources[1:]:
            block_end = source + keep * block_end
        ends = lax.all_to_all(block_end, "tm", split_axis=0, concat_axis=0, tiled=True)
        ends = ends.reshape(tm_count, share, narrow)
        last = ends[0]
        for k in range(1, tm_count):
            last = ends[k] + block_keep * last
        entry = [closing * last]
        for k in range(tm_count - 1):
            entry.append(ends[k] + block_keep * entry[k])
        entry = jnp.concatenate(entry, 0)
        carry = lax.all_to_all(entry, "tm", split_axis=0, concat_axis=0, tiled=True)
        wrapped = carry
        solved = []
        for source in sources:
            carry = source + keep * carry
            solved.append(carry)
        field = table_times(rows_in, jnp.stack(solved, 0))
        field = lax.all_to_all(field, "rows", split_axis=1, concat_axis=2, tiled=True)
        update = times_table(field.reshape(steps * strip, width), columns_in)
        if sweep == 0:
            last_grid, last_div = start, start_div
        else:
            last_grid, last_div = grid, div
        warmth = warmth + update.reshape(steps, strip, width)
    return warmth


def solution(mesh):
    in_specs = (P("rows", None), P("tm", None, None), P(), P(), P(), P())
    out_specs = P("tm", "rows", None)
    return jax.shard_map(shards, mesh=mesh, in_specs=in_specs, out_specs=out_specs, check_vma=False)
```

time: 824 us -> 394 us (0.48)
  matrix products: 212 us -> 0 us
  local copies, waits for them, and re-layouts: 224 us -> 46.4 us
  blocking collectives: 269 us -> 114 us
  Pallas kernels: 0 us -> 62.7 us
  waiting for transfers between devices: 44.3 us -> 101 us
    dot_general x12 -> x0, matrix products: 212 us -> none  [the longest x4 128 us: along_rows(): return jnp.einsum('kn,afnc->afkc', table, values, precision=HIGHEST)]
    all_to_all x6 -> x4, blocking collectives: 269 us -> 114 us  [the longest x2 56.3 us: shards(): lax.all_to_all(field, 'rows', split_axis=1, concat_axis=2, tiled=True)]
    all_to_all x2 -> x4, waiting for transfers between devices: 24.7 us -> 101 us  [the longest x2 50 us: shards(): lax.all_to_all(modes.reshape(steps, strip, width), 'rows', split_axis=2,...]
    dot_general x14 -> x0, local copies, waits for them, and re-layouts: 76 us -> none  [the longest x6 45.7 us: fourier_inverse(): jnp.dot(table, values.reshape(2 * count, -1), precision=HIGHEST, preferre...]
    pallas_call x0 -> x9, Pallas kernels: none -> 62.7 us  [the longest x4 30.3 us: times_table(): pl.pallas_call(columns_kernel, grid=(width // block,), out_shape=jax.Shap...]
    reshape x4 -> x3, local copies, waits for them, and re-layouts: 36.3 us -> 8.88 us  [the longest x2 8.22 us: shards(): modes.reshape(steps, strip, width)]
    broadcast_in_dim x30 -> x2, local copies, waits for them, and re-layouts: 27.3 us -> 0.66 us  [the longest x1 0.33 us: shards(): base = jnp.repeat(base_tiles, TILE, axis=1)[None]]
    transpose x2 -> x0, local copies, waits for them, and re-layouts: 20.9 us -> none  [along_rows(): return jnp.einsum('kn,afnc->afkc', table, values, precision=HIGHEST)]
  transfers between devices with their start and end apart: 8 -> 8, of which waited for: 3 -> 5; matrix products, arithmetic and copies ran while one was open for 11% -> 4% of each run, Pallas kernels for 0% -> 1%
where the time goes in v1:
time: 394 us; the launch traced here: 392 us
  blocking collectives  114 us (29%)
  waiting for transfers between devices  101 us (26%)
  Pallas kernels  62.7 us (16%)
  local copies, waits for them, and re-layouts  46.4 us (12%)
  other arithmetic  39.4 us (10%)
  starting transfers between devices  27.6 us (7%)
    all_to_all x2, blocking collectives, shards(): lax.all_to_all(field, 'rows', split_axis=1, concat_axis=2, tiled=True)  56.3 us
    all_to_all x2, waiting for transfers between devices, shards(): lax.all_to_all(modes.reshape(steps, strip, width), 'rows', split_axis=2,...  50 us
    pallas_call x4, Pallas kernels, times_table(): pl.pallas_call(columns_kernel, grid=(width // block,), out_shape=jax.Shap...  30.3 us
    pallas_call x4, Pallas kernels, table_times(): pl.pallas_call(rows_kernel, grid=(height // block,), out_shape=jax.ShapeD...  29.8 us
    all_to_all x1, blocking collectives, shards(): carry = lax.all_to_all(entry, 'tm', split_axis=0, concat_axis=0, tiled=True)  28.9 us
    all_to_all x1, blocking collectives, shards(): lax.all_to_all(block_end, 'tm', split_axis=0, concat_axis=0, tiled=True)  28.5 us
    all_to_all x1, waiting for transfers between devices, shards(): lax.all_to_all(block_end, 'tm', split_axis=0, concat_axis=0, tiled=True)  25.6 us
    all_to_all x1, waiting for transfers between devices, shards(): carry = lax.all_to_all(entry, 'tm', split_axis=0, concat_axis=0, tiled=True)  25.4 us
  transfers between devices with their start and end apart: 8, of which 5 were waited for; matrix products, arithmetic and copies ran while one was open for 4% of the time, Pallas kernels for 1%

profile of v1, /device:TPU:0, one launch (start us, length us, event | category | flops | bytes accessed | tf_op | source)
XLA Modules:
  0.0 392.1 jit_solution(3354852746309055998)
XLA Ops:
  0.8 1.3 collective-permute-start.1
  2.1 3.0 collective-permute-start
  5.2 1.5 fusion.64
  6.7 1.5 fusion.63
  8.2 1.7 gather_fusion
  9.9 2.6 select_select_fusion
  12.5 2.5 select_select_fusion.1
  17.4 1.2 broadcast_in_dim_reshape.7
  18.6 2.6 shard_map.100
  21.2 2.6 fusion.41
  25.2 1.0 copy-done.11
  26.7 1.6 bitcast_add_fusion.x_ref
  28.3 7.6 %shard_map.101 = f32[512,1024]{1,0:T(8,128)} custom-call(f32[512,1024]{1,0:T(8,128)} %bitcast_add_fusion.x_ref, bf16[1024,1024]{1,0:T(8,128)(2,1)} %constant.63.clone.high_ref, bf16[1024,1024]{1,0:T(8,128)(2,1)} %constant.64.clone.low_ref), custom_call_target="tpu_custom_call" | custom-call | tf_op jit(solution)/shard_map/pallas_call | solution.py:68
  35.9 4.1 %copy.19 = f32[2,256,1024]{1,0,2:T(2,128)} copy(f32[2,256,1024]{2,1,0:T(8,128)} %bitcast.243) | data formatting | bytes 4194304 | tf_op jit(solution)/shard_map/reshape | solution.py:235
  40.0 4.4 %all-to-all-start = ((f32[2,256,1024]{1,0,2:T(2,128)}), f32[2,256,1024]{1,0,2:T(2,128)S(1)}, u32[]{:S(2)}, u32[]{:S(2)}) async-start(f32[2,256,1024]{1,0,2:T(2,128)} %copy.19), calls=%async_computation | async-start | bytes 4194304 | tf_op jit(solution)/shard_map/all_to_all | solution.py:234
  45.7 24.3 %all-to-all-done = f32[2,256,1024]{1,0,2:T(2,128)S(1)} async-done(((f32[2,256,1024]{1,0,2:T(2,128)}), f32[2,256,1024]{1,0,2:T(2,128)S(1)}, u32[]{:S(2)}, u32[]{:S(2)}) %all-to-all-start) | async-done | bytes 2097184 | tf_op jit(solution)/shard_map/all_to_all | solution.py:234
  70.1 1.5 copy.20
  71.5 2.9 copy.21
  74.5 7.5 %shard_map.102 = f32[2,1024,256]{2,1,0:T(8,128)} custom-call(bf16[1024,1024]{1,0:T(8,128)(2,1)} %constant.65.clone.high_ref, bf16[1024,1024]{1,0:T(8,128)(2,1)} %constant.124.clone.low_ref, f32[2,1024,256]{2,1,0:T(8,128)} %bitcast.244), custom_call_target="tpu_custom_call" | custom-call | tf_op jit(solution)/shard_map/pallas_call | solution.py:99
  81.9 1.7 fusion.61
  83.6 1.5 fusion.27
  85.1 6.6 %all-to-all-start.1 = ((f32[8,128,256]{2,1,0:T(8,128)}), f32[8,128,256]{2,1,0:T(8,128)S(1)}, u32[]{:S(2)}, u32[]{:S(2)}) async-start(f32[8,128,256]{2,1,0:T(8,128)} %fusion.27), calls=%async_computation.1 | async-start | bytes 2097152 | tf_op jit(solution)/shard_map/all_to_all | solution.py:245
  91.7 25.6 %all-to-all-done.1 = f32[8,128,256]{2,1,0:T(8,128)S(1)} async-done(((f32[8,128,256]{2,1,0:T(8,128)}), f32[8,128,256]{2,1,0:T(8,128)S(1)}, u32[]{:S(2)}, u32[]{:S(2)}) %all-to-all-start.1) | async-done | bytes 1048608 | tf_op jit(solution)/shard_map/all_to_all | solution.py:245
  118.4 1.2 constant_dynamic-update-slice_fusion.2
  119.6 1.0 constant_dynamic-update-slice_fusion.1
  120.6 1.1 constant_dynamic-update-slice_fusion
  121.7 1.2 add_dynamic-update-slice_fusion.1
  122.9 1.0 copy-done.15
  123.9 4.3 %all-to-all-start.2 = ((f32[8,128,256]{2,1,0:T(8,128)}), f32[8,128,256]{2,1,0:T(8,128)}, u32[]{:S(2)}, u32[]{:S(2)}) async-start(f32[8,128,256]{2,1,0:T(8,128)} %bitcast.257), calls=%async_computation.2 | async-start | bytes 2097152 | tf_op jit(solution)/shard_map/all_to_all | solution.py:254
  128.2 25.4 %all-to-all-done.2 = f32[8,128,256]{2,1,0:T(8,128)} async-done(((f32[8,128,256]{2,1,0:T(8,128)}), f32[8,128,256]{2,1,0:T(8,128)}, u32[]{:S(2)}, u32[]{:S(2)}) %all-to-all-start.2) | async-done | bytes 1048608 | tf_op jit(solution)/shard_map/all_to_all | solution.py:254
  153.6 1.8 fusion.20
  155.4 1.5 pad_maximum_fusion.1.x_ref
  156.9 7.5 %shard_map.103 = f32[2,1024,256]{2,1,0:T(8,128)} custom-call(bf16[1024,1024]{1,0:T(8,128)(2,1)} %constant.63.clone.high_ref, bf16[1024,1024]{1,0:T(8,128)(2,1)} %constant.64.clone.low_ref, f32[2,1024,256]{2,1,0:T(8,128)} %pad_maximum_fusion.1.x_ref), custom_call_target="tpu_custom_call" | custom-call | tf_op jit(solution)/shard_map/pallas_call | solution.py:99
  164.3 3.2 copy.22
  167.5 28.1 %all_to_all.102 = f32[2,1024,256]{2,0,1:T(2,128)S(1)} all-to-all(f32[2,1024,256]{2,0,1:T(2,128)S(1)} %copy.22), channel_id=1, replica_groups=mesh['tm'=8,'rows'=4] {'rows'}, dimensions={1} | all-to-all | bytes 4194304 | tf_op jit(solution)/shard_map/all_to_all | solution.py:261
  195.7 1.4 copy.23
  197.0 1.8 copy.29
  198.8 7.6 %shard_map.104 = f32[512,1024]{1,0:T(8,128)} custom-call(f32[512,1024]{1,0:T(8,128)} %bitcast.245, bf16[1024,1024]{1,0:T(8,128)(2,1)} %constant.65.clone.high_ref, bf16[1024,1024]{1,0:T(8,128)(2,1)} %constant.124.clone.low_ref), custom_call_target="tpu_custom_call" | custom-call | tf_op jit(solution)/shard_map/pallas_call | solution.py:68
  206.4 2.0 broadcast_add_fusion
  208.4 1.4 collective-permute-start.3
  209.8 3.0 collective-permute-start.2
  215.7 1.2 fusion.9
  217.0 1.0 fusion.3
  218.2 2.7 fusion.7
  220.9 7.5 %shard_map.105 = f32[512,1024]{1,0:T(8,128)} custom-call(f32[512,1024]{1,0:T(8,128)} %bitcast.234, bf16[1024,1024]{1,0:T(8,128)(2,1)} %constant.63.clone.high_ref, bf16[1024,1024]{1,0:T(8,128)(2,1)} %constant.64.clone.low_ref), custom_call_target="tpu_custom_call" | custom-call | tf_op jit(solution)/shard_map/pallas_call | solution.py:68
  228.4 4.1 %copy.24 = f32[2,256,1024]{1,0,2:T(2,128)} copy(f32[2,256,1024]{2,1,0:T(8,128)} %bitcast.246) | data formatting | bytes 4194304 | tf_op jit(solution)/shard_map/reshape | solution.py:235
  232.6 3.6 all-to-all-start.4
  236.2 25.6 %all-to-all-done.4 = f32[2,256,1024]{1,0,2:T(2,128)S(1)} async-done(((f32[2,256,1024]{1,0,2:T(2,128)}), f32[2,256,1024]{1,0,2:T(2,128)S(1)}, u32[]{:S(2)}, u32[]{:S(2)}) %all-to-all-start.4) | async-done | bytes 2097184 | tf_op jit(solution)/shard_map/all_to_all | solution.py:234
  261.8 1.5 copy.25
  263.3 2.9 copy.26
  266.2 7.5 %shard_map.106 = f32[2,1024,256]{2,1,0:T(8,128)} custom-call(bf16[1024,1024]{1,0:T(8,128)(2,1)} %constant.65.clone.high_ref, bf16[1024,1024]{1,0:T(8,128)(2,1)} %constant.124.clone.low_ref, f32[2,1024,256]{2,1,0:T(8,128)} %bitcast.247), custom_call_target="tpu_custom_call" | custom-call | tf_op jit(solution)/shard_map/pallas_call | solution.py:99
  273.6 1.7 fusion.59
  275.3 1.8 fusion.31
  277.1 28.5 %all_to_all.103 = f32[8,128,256]{2,1,0:T(8,128)S(1)} all-to-all(f32[8,128,256]{2,1,0:T(8,128)S(1)} %fusion.31), channel_id=1, replica_groups=mesh['tm'=8,'rows'=4] {'tm'}, dimensions={0} | all-to-all | bytes 2097152 | tf_op jit(solution)/shard_map/all_to_all | solution.py:245
  306.7 28.9 %all_to_all.104 = f32[8,128,256]{2,1,0:T(8,128)S(1)} all-to-all(f32[8,128,256]{2,1,0:T(8,128)S(1)} %bitcast.258), channel_id=1, replica_groups=mesh['tm'=8,'rows'=4] {'tm'}, dimensions={0} | all-to-all | bytes 2097152 | tf_op jit(solution)/shard_map/all_to_all | solution.py:254
  335.6 1.9 fusion.25
  337.5 1.5 pad_maximum_fusion.2.x_ref
  338.9 7.4 %shard_map.107 = f32[2,1024,256]{2,1,0:T(8,128)} custom-call(bf16[1024,1024]{1,0:T(8,128)(2,1)} %constant.63.clone.high_ref, bf16[1024,1024]{1,0:T(8,128)(2,1)} %constant.64.clone.low_ref, f32[2,1024,256]{2,1,0:T(8,128)} %pad_maximum_fusion.2.x_ref), custom_call_target="tpu_custom_call" | custom-call | tf_op jit(solution)/shard_map/pallas_call | solution.py:99
  346.4 3.2 copy.27
  349.6 28.2 %all_to_all.105 = f32[2,1024,256]{2,0,1:T(2,128)S(1)} all-to-all(f32[2,1024,256]{2,0,1:T(2,128)S(1)} %copy.27), channel_id=1, replica_groups=mesh['tm'=8,'rows'=4] {'rows'}, dimensions={1} | all-to-all | bytes 4194304 | tf_op jit(solution)/shard_map/all_to_all | solution.py:261
  377.8 1.4 copy.28
  379.1 1.8 copy.32
  380.9 7.7 %shard_map.108 = f32[512,1024]{1,0:T(8,128)} custom-call(f32[512,1024]{1,0:T(8,128)} %bitcast.242, bf16[1024,1024]{1,0:T(8,128)(2,1)} %constant.65.clone.high_ref, bf16[1024,1024]{1,0:T(8,128)(2,1)} %constant.124.clone.low_ref), custom_call_target="tpu_custom_call" | custom-call | tf_op jit(solution)/shard_map/pallas_call | solution.py:68
  388.6 3.5 fusion.65
  (74 shorter events, 11.1 us)
Async XLA Ops:
  0.0 15.0 %copy-start = (s32[2,8,8]{2,1,0:T(8,128)S(1)}, s32[2,8,8]{2,1,0:T(8,128)}, u32[]{:S(2)}) copy-start(s32[2,8,8]{2,1,0:T(8,128)} %param.11) | copy-start | bytes 1540
  0.8 20.4 %collective-permute-start.1 = (f32[1,1,1024]{2,1,0:T(1,128)S(1)}, f32[1,1,1024]{2,1,0:T(1,128)S(1)}, u32[]{:S(2)}, u32[]{:S(2)}) collective-permute-start(f32[1,1,1024]{2,1,0:T(1,128)S(1)} %get-tuple-element.37), channel_id=1, source_target_pairs={{1,0},{2,1},{3,2},{5,4},{6,5},{7,6},{9,8},{10,9},{11,10},{13,12},{... | collective-permute-start | bytes 12296 | tf_op jit(solution)/shard_map/ppermute | solution.py:27
  2.1 19.1 %collective-permute-start = (f32[1,1,1024]{2,1,0:T(1,128)S(1)}, f32[1,1,1024]{2,1,0:T(1,128)S(1)}, u32[]{:S(2)}, u32[]{:S(2)}) collective-permute-start(f32[1,1,1024]{2,1,0:T(1,128)S(1)} %get-tuple-element.36), channel_id=1, source_target_pairs={{0,1},{1,2},{2,3},{4,5},{5,6},{6,7},{8,9},{9,10},{10,11},{12,13},{... | collective-permute-start | bytes 12296 | tf_op jit(solution)/shard_map/ppermute | solution.py:24
  16.1 1.0 copy-start.7
  17.4 3.8 copy-start.9
  17.4 3.8 copy-start.2
  24.8 2.0 copy-start.13
  25.2 1.0 copy-start.11
  40.0 4.4 %copy-start.16 = (f32[4]{0:T(128)S(1)}, f32[4]{0:T(128)}, u32[]{:S(2)}) copy-start(f32[4]{0:T(128)} %param.14) | copy-start | bytes 52
  40.0 30.1 %all-to-all-start = ((f32[2,256,1024]{1,0,2:T(2,128)}), f32[2,256,1024]{1,0,2:T(2,128)S(1)}, u32[]{:S(2)}, u32[]{:S(2)}) async-start(f32[2,256,1024]{1,0,2:T(2,128)} %copy.19), calls=%async_computation | async-start | bytes 4194304 | tf_op jit(solution)/shard_map/all_to_all | solution.py:234
  85.1 32.2 %all-to-all-start.1 = ((f32[8,128,256]{2,1,0:T(8,128)}), f32[8,128,256]{2,1,0:T(8,128)S(1)}, u32[]{:S(2)}, u32[]{:S(2)}) async-start(f32[8,128,256]{2,1,0:T(8,128)} %fusion.27), calls=%async_computation.1 | async-start | bytes 2097152 | tf_op jit(solution)/shard_map/all_to_all | solution.py:245
  117.3 1.0 copy-start.6
  118.4 35.3 %copy-start.5 = (f32[2,1024,256]{2,1,0:T(8,128)S(1)}, f32[2,1024,256]{2,1,0:T(8,128)}, u32[]{:S(2)}) copy-start(f32[2,1024,256]{2,1,0:T(8,128)} %shard_map.102) | copy-start | bytes 6291460
  122.9 1.0 copy-start.15
  123.9 29.7 %all-to-all-start.2 = ((f32[8,128,256]{2,1,0:T(8,128)}), f32[8,128,256]{2,1,0:T(8,128)}, u32[]{:S(2)}, u32[]{:S(2)}) async-start(f32[8,128,256]{2,1,0:T(8,128)} %bitcast.257), calls=%async_computation.2 | async-start | bytes 2097152 | tf_op jit(solution)/shard_map/all_to_all | solution.py:254
  206.4 6.5 %copy-start.10 = (f32[258,8,128]{2,1,0:T(8,128)S(1)}, f32[258,8,128]{2,1,0:T(8,128)}, u32[]{:S(2)}) copy-start(f32[258,8,128]{2,1,0:T(8,128)} %copy-done.9) | copy-start | bytes 3170308
  208.4 4.6 %copy-start.8 = (f32[258,8,128]{2,1,0:T(8,128)S(1)}, f32[258,8,128]{2,1,0:T(8,128)}, u32[]{:S(2)}) copy-start(f32[258,8,128]{2,1,0:T(8,128)} %copy-done.7) | copy-start | bytes 3170308
  208.4 5.1 %collective-permute-start.3 = (f32[2,1,1024]{2,1,0:T(1,128)S(1)}, f32[2,1,1024]{2,1,0:T(1,128)S(1)}, u32[]{:S(2)}, u32[]{:S(2)}) collective-permute-start(f32[2,1,1024]{2,1,0:T(1,128)S(1)} %get-tuple-element.31), channel_id=1, source_target_pairs={{1,0},{2,1},{3,2},{5,4},{6,5},{7,6},{9,8},{10,9},{11,10},{13,12},{... | collective-permute-start | bytes 24584 | tf_op jit(solution)/shard_map/ppermute | solution.py:27
  209.8 3.8 collective-permute-start.2
  213.1 1.2 copy-start.14
  216.9 1.2 copy-start.12
  232.6 29.2 %all-to-all-start.4 = ((f32[2,256,1024]{1,0,2:T(2,128)}), f32[2,256,1024]{1,0,2:T(2,128)S(1)}, u32[]{:S(2)}, u32[]{:S(2)}) async-start(f32[2,256,1024]{1,0,2:T(2,128)} %copy.24), calls=%async_computation.4 | async-start | bytes 4194304 | tf_op jit(solution)/shard_map/all_to_all | solution.py:234
  306.2 29.4 %copy-start.4 = (f32[2,1024,256]{2,1,0:T(8,128)S(1)}, f32[2,1024,256]{2,1,0:T(8,128)}, u32[]{:S(2)}) copy-start(f32[2,1024,256]{2,1,0:T(8,128)} %shard_map.106) | copy-start | bytes 6291460
  380.9 7.7 %copy-start.3 = (f32[512,1024]{1,0:T(8,128)S(1)}, f32[512,1024]{1,0:T(8,128)}, u32[]{:S(2)}) copy-start(f32[512,1024]{1,0:T(8,128)} %shard_map.104) | copy-start | bytes 6291460
  388.6 3.5 copy-start.1
